TPU v7x, 512 devices: a whole 4x8x8 slice. The times are simulated.
512 devices in a mesh: ta: 64 (over y, x, core), gz: 8 (over z).
Axes of the slice: x: 4, y: 8, z: 8, core: 2. Of those that a mesh axis runs over, the one named last changes fastest.
Arguments:
- time_links: float32 [2, 3, 3, 128, 32, 256], P(None, None, None, 'ta', 'gz'), may hold values from -1 to 1, as said below
- space_links: float32 [3, 2, 3, 3, 128, 32, 256], P(None, None, None, None, 'ta', 'gz'), may hold values from -1 to 1, as said below
Outputs:
- gauge: float32 [2, 3, 3, 128, 32, 256], P(None, None, None, 'ta', 'gz')
- links_fixed: float32 [3, 2, 3, 3, 128, 32, 256], P(None, None, None, None, 'ta', 'gz')
- action_profile: float32 [128, 32], P('ta', 'gz')
- action_mean: float32 [], replicated
Inputs may be any that keep to these rules, and one draw needn't show every extreme that they name: `time_links`: every 3 x 3 complex matrix is unitary up to float32 rounding. `space_links`: every 3 x 3 complex matrix is unitary up to float32 rounding.
All inputs are finite; a program needn't handle non-finite values.
Results may differ from a plain program's by a relative error of at most 0.00024.
Values sent between devices are 32-bit elements; how exact they have to be, the bound alone decides.
A program may use at most 64 MiB of HBM per device.

v0:
```python
import jax
import jax.numpy as jnp
from jax import lax
from jax.sharding import Mesh
from jax.sharding import PartitionSpec as P

X = 16
Y = 16
TA = ("ta_0", "ta_1", "ta_2")
TA_GZ = ("ta_0", "ta_1", "ta_2", "gz")


def filled_with(shard, identity):
    return jnp.broadcast_to(jnp.asarray(identity, shard.dtype), shard.shape)


def carried_in(shard, axes, combine, identity):
    before = start = filled_with(shard, identity)
    so_far = shard
    for axis in reversed(axes):
        length, mine = (lax.axis_size(axis), lax.axis_index(axis))
        pieces = lax.all_gather(so_far, axis)
        inside, so_far = (start, start)
        for k in range(length):
            passed = k < mine
            so_far = combine(so_far, pieces[k])
            inside = jnp.where(passed, so_far, inside)
        before = combine(inside, before)
    return before


def from_behind(block, axis, distance):
    devices = range(lax.axis_size(axis))
    route = [((i - distance) % len(devices), i) for i in devices]
    return lax.ppermute(block, axis, route)


def over_axes(shard, axes):
    for axis in axes:
        shard = lax.psum(shard, axis)
    return shard


def complex_product(first_pair, second_pair):
    first_real, first_imag = first_pair
    second_real, second_imag = second_pair
    real_part = jnp.sum(
        first_real[:, :, None] * second_real[None] - first_imag[:, :, None] * second_imag[None],
        axis=1,
    )
    imag_part = jnp.sum(
        first_real[:, :, None] * second_imag[None] + first_imag[:, :, None] * second_real[None],
        axis=1,
    )
    return (real_part, imag_part)


def dagger(matrix_pair):
    return (jnp.swapaxes(matrix_pair[0], 0, 1), -jnp.swapaxes(matrix_pair[1], 0, 1))


def plane_step(matrix_pair, direction):

    def shifted(values):
        leading = values.shape[:-1]
        lattice_grid = values.reshape(leading + (X, Y))
        lattice_grid = jnp.roll(lattice_grid, -1, axis=lattice_grid.ndim - 2 + direction)
        return lattice_grid.reshape(leading + (X * Y,))

    return (shifted(matrix_pair[0]), shifted(matrix_pair[1]))


def upward_z(matrix_pair, upper_layer):
    return (
        jnp.concatenate([matrix_pair[0][..., 1:, :], upper_layer[0]], axis=-2),
        jnp.concatenate([matrix_pair[1][..., 1:, :], upper_layer[1]], axis=-2),
    )


def plaquette_density(link_set, forward_x, forward_y):
    forward_z = [forward_x, forward_y]
    terms = []
    for first_dir, second_dir in ((0, 1), (0, 2), (1, 2)):
        along_first = link_set[first_dir]
        along_second = link_set[second_dir]
        second_moved = plane_step(along_second, first_dir)
        if second_dir < 2:
            first_moved = plane_step(along_first, second_dir)
        else:
            first_moved = forward_z[first_dir]
        loop_matrix = complex_product(
            complex_product(along_first, second_moved),
            complex_product(dagger(first_moved), dagger(along_second)),
        )
        trace_real = loop_matrix[0][0, 0] + loop_matrix[0][1, 1] + loop_matrix[0][2, 2]
        terms.append(1.0 - trace_real / 3.0)
    return terms[0] + terms[1] + terms[2]


def on_device(time_links, space_links):
    local_steps = time_links.shape[3]
    layer_count = time_links.shape[4]
    site_count = time_links.shape[5]
    unit_matrix = jnp.eye(3, dtype=jnp.float32)[:, :, None, None]
    unit_real = jnp.broadcast_to(unit_matrix, (3, 3, layer_count, site_count))
    running = (unit_real, jnp.zeros_like(unit_real))
    prefixes = []
    for step_index in range(local_steps):
        prefixes.append(running)
        running = complex_product(
            running, (time_links[0, :, :, step_index], time_links[1, :, :, step_index])
        )

    def combine(earlier, later):
        return jnp.stack(complex_product((earlier[0], earlier[1]), (later[0], later[1])))

    identity_pair = jnp.stack([unit_real, jnp.zeros_like(unit_real)])
    carried = carried_in(jnp.stack(running), TA, combine, identity_pair)
    carried_pair = (carried[0], carried[1])
    time_slices = [complex_product(carried_pair, prefix_pair) for prefix_pair in prefixes]
    gauge_pair = (
        jnp.stack([piece[0] for piece in time_slices], axis=2),
        jnp.stack([piece[1] for piece in time_slices], axis=2),
    )
    first_layer = jnp.stack([gauge_pair[0][..., 0:1, :], gauge_pair[1][..., 0:1, :]])
    gauge_above = from_behind(first_layer, "gz", -1)
    gauge_next_z = upward_z(gauge_pair, (gauge_above[0], gauge_above[1]))
    fixed = []
    for direction in range(3):
        link_pair = (space_links[direction, 0], space_links[direction, 1])
        ahead = plane_step(gauge_pair, direction) if direction < 2 else gauge_next_z
        fixed.append(complex_product(complex_product(gauge_pair, link_pair), dagger(ahead)))
    links_fixed = jnp.stack([jnp.stack(pair) for pair in fixed])
    top_layers = jnp.stack(
        [jnp.stack([pair[0][..., 0:1, :], pair[1][..., 0:1, :]]) for pair in fixed[:2]]
    )
    layers_above = from_behind(top_layers, "gz", -1)
    forward_x = upward_z(fixed[0], (layers_above[0, 0], layers_above[0, 1]))
    forward_y = upward_z(fixed[1], (layers_above[1, 0], layers_above[1, 1]))
    density = plaquette_density(fixed, forward_x, forward_y)
    action_profile = jnp.mean(density, axis=-1) / 3.0
    local_total = jnp.sum(action_profile)
    whole_total = over_axes(local_total, TA_GZ)
    action_mean = whole_total / (action_profile.size * lax.axis_size(TA) * lax.axis_size("gz"))
    return (jnp.stack(gauge_pair), links_fixed, action_profile, action_mean)


def solution(mesh):
    finer = Mesh(mesh.devices.reshape(8, 4, 2, mesh.shape["gz"]), ("ta_0", "ta_1", "ta_2", "gz"))
    placed = (P(None, None, None, TA, "gz", None), P(None, None, None, None, TA, "gz", None))
    return jax.shard_map(
        on_device,
        mesh=finer,
        in_specs=placed,
        out_specs=(
            P(None, None, None, TA, "gz", None),
            P(None, None, None, None, TA, "gz", None),
            P(TA, "gz"),
            P(),
        ),
        check_vma=False,
    )
```

profile of v0, /device:TPU:8, one launch (start us, length us, event | category | flops | bytes accessed | tf_op | source)
XLA Modules:
  0.0 155.2 jit_solution(9629887027639376099)
XLA Ops:
  0.6 0.9 broadcast_multiply_fusion.10
  1.9 1.9 %all-gather = f32[4,3,3,4,256]{4,3,2,1,0:T(4,128)S(1)} all-gather(f32[2,3,3,4,256]{4,3,2,1,0:T(4,128)S(1)} %pad_maximum_fusion.13), channel_id=2, replica_groups=mesh['ta_0'=8,'ta_1'=4,'ta_2'=2,'gz'=8] {'ta_2'}, dimensions={0}, use_global_device_ids=true | all-gather | bytes 221184 | tf_op jit(solution)/shard_map/all_gather | solution.py:22
  4.2 12.7 %all-gather.1 = f32[8,3,3,4,256]{4,3,2,1,0:T(4,128)S(1)} all-gather(f32[2,3,3,4,256]{4,3,2,1,0:T(4,128)S(1)} %get-tuple-element.165), channel_id=3, replica_groups=mesh['ta_0'=8,'ta_1'=4,'ta_2'=2,'gz'=8] {'ta_1'}, dimensions={0}, use_global_device_ids=true | all-gather | bytes 368640 | tf_op jit(solution)/shard_map/all_gather | solution.py:22
  17.4 28.1 %all-gather.2 = f32[16,3,3,4,256]{4,3,2,1,0:T(4,128)S(1)} all-gather(f32[2,3,3,4,256]{4,3,2,1,0:T(4,128)S(1)} %get-tuple-element.159), channel_id=4, replica_groups=mesh['ta_0'=8,'ta_1'=4,'ta_2'=2,'gz'=8] {'ta_0'}, dimensions={0}, use_global_device_ids=true | all-gather | bytes 663552 | tf_op jit(solution)/shard_map/all_gather | solution.py:22
  47.8 9.2 %collective-permute-start = (f32[2,3,3,2,1,256]{5,3,2,1,4,0:T(2,128)}, f32[2,3,3,2,1,256]{5,3,2,1,4,0:T(2,128)}, u32[]{:S(2)}, u32[]{:S(2)}) collective-permute-start(f32[2,3,3,2,1,256]{5,3,2,1,4,0:T(2,128)} %pad_maximum_fusion.17), channel_id=1, source_target_pairs={{1,0},{2,1},{3,2},{4,3},{5,4},{6,5},{7,6},{0,7},{9,8},{10,9},{11,1... | collective-permute-start | bytes 110600 | tf_op jit(solution)/shard_map/ppermute | solution.py:35
  60.9 1.0 copy-done.3
  62.1 0.9 neg.62
  63.0 1.5 copy.214
  67.4 0.9 copy-done.7
  68.3 1.2 subtract_reduce_fusion.14
  70.7 2.6 %collective-permute-start.1 = (f32[2,2,3,3,2,1,256]{6,5,4,3,2,1,0:T(1,128)}, f32[2,2,3,3,2,1,256]{6,5,4,3,2,1,0:T(1,128)}, u32[]{:S(2)}, u32[]{:S(2)}) collective-permute-start(f32[2,2,3,3,2,1,256]{6,5,4,3,2,1,0:T(1,128)} %pad_maximum_fusion.16), channel_id=1, source_target_pairs={{1,0},{2,1},{3,2},{4,3},{5,4},{6,5},{7,6},{0,7},{9,8},{10,9},{11,1... | collective-permute-start | bytes 221192 | tf_op jit(solution)/shard_map/ppermute | solution.py:35
  78.5 0.9 copy-done.16
  82.5 0.8 subtract_reduce_fusion.7
  86.0 0.9 mul.1834
  86.9 0.9 mul.1830
  91.7 0.9 slice.517
  93.7 0.9 mul.1880
  101.6 0.8 copy-done.21
  104.2 1.2 fusion.29
  105.4 16.0 %psum.28 = f32[]{:T(128)} all-reduce(f32[]{:T(128)} %get-tuple-element.98), channel_id=1, replica_groups=mesh['ta_0'=8,'ta_1'=4,'ta_2'=2,'gz'=8] {'ta_0'}, use_global_device_ids=true, to_apply=%region_71.72 | all-reduce | flops 1 | bytes 8 | tf_op jit(solution)/shard_map/psum | solution.py:40
  122.1 11.1 %psum.29 = f32[]{:T(128)} all-reduce(f32[]{:T(128)} %psum.28), channel_id=1, replica_groups=mesh['ta_0'=8,'ta_1'=4,'ta_2'=2,'gz'=8] {'ta_1'}, use_global_device_ids=true, to_apply=%region_72.73 | all-reduce | flops 1 | bytes 8 | tf_op jit(solution)/shard_map/psum | solution.py:40
  133.2 3.1 %psum.30 = f32[]{:T(128)} all-reduce(f32[]{:T(128)} %psum.29), channel_id=1, replica_groups=mesh['ta_0'=8,'ta_1'=4,'ta_2'=2,'gz'=8] {'ta_2'}, use_global_device_ids=true, to_apply=%region_73.74 | all-reduce | flops 1 | bytes 8 | tf_op jit(solution)/shard_map/psum | solution.py:40
  136.3 0.9 pad_maximum_fusion.9
  137.2 16.2 %psum.31 = f32[]{:T(128)} all-reduce(f32[]{:T(128)} %psum.30), channel_id=1, replica_groups=mesh['ta_0'=8,'ta_1'=4,'ta_2'=2,'gz'=8] {'gz'}, use_global_device_ids=true, to_apply=%region_74.75 | all-reduce | flops 1 | bytes 8 | tf_op jit(solution)/shard_map/psum | solution.py:40
  (197 shorter events, 36.6 us)
Async XLA Ops:
  0.6 0.9 copy-start.4
  47.8 40.0 %collective-permute-start = (f32[2,3,3,2,1,256]{5,3,2,1,4,0:T(2,128)}, f32[2,3,3,2,1,256]{5,3,2,1,4,0:T(2,128)}, u32[]{:S(2)}, u32[]{:S(2)}) collective-permute-start(f32[2,3,3,2,1,256]{5,3,2,1,4,0:T(2,128)} %pad_maximum_fusion.17), channel_id=1, source_target_pairs={{1,0},{2,1},{3,2},{4,3},{5,4},{6,5},{7,6},{0,7},{9,8},{10,9},{11,1... | collective-permute-start | bytes 110600 | tf_op jit(solution)/shard_map/ppermute | solution.py:35
  60.8 1.0 copy-start.3
  67.4 0.9 copy-start.7
  67.4 0.9 copy-start.8
  68.3 1.2 copy-start.14
  70.7 29.0 %collective-permute-start.1 = (f32[2,2,3,3,2,1,256]{6,5,4,3,2,1,0:T(1,128)}, f32[2,2,3,3,2,1,256]{6,5,4,3,2,1,0:T(1,128)}, u32[]{:S(2)}, u32[]{:S(2)}) collective-permute-start(f32[2,2,3,3,2,1,256]{6,5,4,3,2,1,0:T(1,128)} %pad_maximum_fusion.16), channel_id=1, source_target_pairs={{1,0},{2,1},{3,2},{4,3},{5,4},{6,5},{7,6},{0,7},{9,8},{10,9},{11,1... | collective-permute-start | bytes 221192 | tf_op jit(solution)/shard_map/ppermute | solution.py:35
  78.4 0.9 copy-start.16
  78.4 0.9 copy-start.17
  81.6 0.9 copy-start.15
  86.9 1.8 %copy-start.13 = (f32[3,3,2,3,256]{4,3,1,0,2:T(4,128)S(1)}, f32[3,3,2,3,256]{4,3,1,0,2:T(4,128)}, u32[]{:S(2)}) copy-start(f32[3,3,2,3,256]{4,3,1,0,2:T(4,128)} %fusion.1) | copy-start | bytes 165892
  88.6 0.9 copy-start.5
  88.6 0.9 copy-start.6
  94.9 1.1 copy-start
  94.9 1.1 copy-start.29
  96.9 0.9 copy-start.20
  97.8 0.9 copy-start.12
  98.7 0.9 copy-start.19
  99.7 0.9 copy-start.23
  100.6 0.9 copy-start.22
  101.5 0.9 copy-start.21
  102.4 0.9 copy-start.10
  104.0 17.4 %copy-start.2 = (f32[2,3,3,2,4,256]{5,4,2,1,3,0:T(4,128)S(1)}, f32[2,3,3,2,4,256]{5,4,2,1,3,0:T(4,128)}, u32[]{:S(2)}) copy-start(f32[2,3,3,2,4,256]{5,4,2,1,3,0:T(4,128)} %pad_maximum_fusion.10) | copy-start | bytes 442372
  133.2 3.2 %copy-start.1 = (f32[1,2,3,3,2,4,256]{6,5,4,3,2,1,0:T(4,128)S(1)}, f32[1,2,3,3,2,4,256]{6,5,4,3,2,1,0:T(4,128)}, u32[]{:S(2)}) copy-start(f32[1,2,3,3,2,4,256]{6,5,4,3,2,1,0:T(4,128)} %maximum_bitcast_fusion) | copy-start | bytes 442372
  (8 other events, 6.5 us)
where the time goes:
time: 156 us; the launch traced here: 155 us
  blocking collectives  89.2 us (57%)
  local copies, waits for them, and re-layouts  33.9 us (22%)
  other arithmetic  17.1 us (11%)
  starting transfers between devices  11.8 us (8%)
  between operations  3.22 us (2%)
    psum x4, blocking collectives, over_axes(): shard = lax.psum(shard, axis)  46.5 us
    all_gather x3, blocking collectives, carried_in(): pieces = lax.all_gather(so_far, axis)  42.7 us
    unnamed x63, local copies, waits for them, and re-layouts  13.1 us
    ppermute x2, starting transfers between devices, from_behind(): return lax.ppermute(block, axis, route)  11.8 us
    slice x18, local copies, waits for them, and re-layouts, shifted(): jnp.roll(lattice_grid, -1, axis=lattice_grid.ndim - 2 + direction)  6.19 us
    reduce_sum x29, other arithmetic, complex_product(): jnp.sum(first_real[:, :, None] * second_real[None] - first_imag[:, :, Non...  6.1 us
    neg x6, local copies, waits for them, and re-layouts, dagger(): -jnp.swapaxes(matrix_pair[1], 0, 1)  3.62 us
  transfers between devices with their start and end apart: 2, of which 0 were waited for; matrix products, arithmetic and copies ran while one was open for 19% of the time, Pallas kernels for 0%

commit v1 on v0

--- a/solution.py
+++ b/solution.py
@@ -37,7 +37,11 @@
 
 def over_axes(shard, axes):
     for axis in axes:
-        shard = lax.psum(shard, axis)
+
+        def place_ladders(x_local, named_axis):
+            return jnp.sum(lax.all_gather(x_local, axis_name=named_axis), 0)
+
+        shard = place_ladders(shard, axis)
     return shard
 
 

time: 156 us -> 167 us (1.071)
  local copies, waits for them, and re-layouts: 33.9 us -> 44.6 us
  blocking collectives: 89.2 us -> 86.6 us
  other arithmetic: 17.1 us -> 18.9 us
    psum x4 -> x0, blocking collectives: 46.5 us -> none  [over_axes(): shard = lax.psum(shard, axis)]
    unnamed x0 -> x4, blocking collectives: none -> 43.9 us
    unnamed x63 -> x73, local copies, waits for them, and re-layouts: 13.1 us -> 23.9 us
    reduce_sum x0 -> x4, other arithmetic: none -> 2.41 us  [place_ladders(): return jnp.sum(lax.all_gather(x_local, axis_name=named_axis), 0)]
  transfers between devices with their start and end apart: 2 -> 2, of which waited for: 0 -> 0; matrix products, arithmetic and copies ran while one was open for 19% -> 20% of each run, Pallas kernels for 0% -> 0%
where the time goes in v1:
time: 167 us; the launch traced here: 165 us
  blocking collectives  86.6 us (52%)
  local copies, waits for them, and re-layouts  44.6 us (27%)
  other arithmetic  18.9 us (11%)
  starting transfers between devices  11.8 us (7%)
  between operations  3.22 us (2%)
    unnamed x4, blocking collectives  43.9 us
    all_gather x3, blocking collectives, carried_in(): pieces = lax.all_gather(so_far, axis)  42.7 us
    unnamed x73, local copies, waits for them, and re-layouts  23.9 us
    ppermute x2, starting transfers between devices, from_behind(): return lax.ppermute(block, axis, route)  11.8 us
    slice x18, local copies, waits for them, and re-layouts, shifted(): jnp.roll(lattice_grid, -1, axis=lattice_grid.ndim - 2 + direction)  6.17 us
    reduce_sum x29, other arithmetic, complex_product(): jnp.sum(first_real[:, :, None] * second_real[None] - first_imag[:, :, Non...  6.1 us
    neg x6, local copies, waits for them, and re-layouts, dagger(): -jnp.swapaxes(matrix_pair[1], 0, 1)  3.64 us
  transfers between devices with their start and end apart: 2, of which 0 were waited for; matrix products, arithmetic and copies ran while one was open for 20% of the time, Pallas kernels for 0%

profile of v1, /device:TPU:8, one launch (start us, length us, event | category | flops | bytes accessed | tf_op | source)
XLA Modules:
  0.0 165.2 jit_solution(12926302872175895109)
XLA Ops:
  1.9 1.9 %all-gather = f32[4,3,3,4,256]{4,3,2,1,0:T(4,128)S(1)} all-gather(f32[2,3,3,4,256]{4,3,2,1,0:T(4,128)S(1)} %pad_maximum_fusion.13), channel_id=2, replica_groups=mesh['ta_0'=8,'ta_1'=4,'ta_2'=2,'gz'=8] {'ta_2'}, dimensions={0}, use_global_device_ids=true | all-gather | bytes 221184 | tf_op jit(solution)/shard_map/all_gather | solution.py:22
  4.2 12.7 %all-gather.1 = f32[8,3,3,4,256]{4,3,2,1,0:T(4,128)S(1)} all-gather(f32[2,3,3,4,256]{4,3,2,1,0:T(4,128)S(1)} %get-tuple-element.165), channel_id=3, replica_groups=mesh['ta_0'=8,'ta_1'=4,'ta_2'=2,'gz'=8] {'ta_1'}, dimensions={0}, use_global_device_ids=true | all-gather | bytes 368640 | tf_op jit(solution)/shard_map/all_gather | solution.py:22
  17.4 28.1 %all-gather.2 = f32[16,3,3,4,256]{4,3,2,1,0:T(4,128)S(1)} all-gather(f32[2,3,3,4,256]{4,3,2,1,0:T(4,128)S(1)} %get-tuple-element.159), channel_id=4, replica_groups=mesh['ta_0'=8,'ta_1'=4,'ta_2'=2,'gz'=8] {'ta_0'}, dimensions={0}, use_global_device_ids=true | all-gather | bytes 663552 | tf_op jit(solution)/shard_map/all_gather | solution.py:22
  47.8 9.2 %collective-permute-start = (f32[2,3,3,2,1,256]{5,3,2,1,4,0:T(2,128)}, f32[2,3,3,2,1,256]{5,3,2,1,4,0:T(2,128)}, u32[]{:S(2)}, u32[]{:S(2)}) collective-permute-start(f32[2,3,3,2,1,256]{5,3,2,1,4,0:T(2,128)} %pad_maximum_fusion.17), channel_id=1, source_target_pairs={{1,0},{2,1},{3,2},{4,3},{5,4},{6,5},{7,6},{0,7},{9,8},{10,9},{11,1... | collective-permute-start | bytes 110600 | tf_op jit(solution)/shard_map/ppermute | solution.py:35
  60.9 1.0 copy-done.2
  63.0 1.5 copy.214
  68.3 1.2 subtract_reduce_fusion.14
  70.7 2.6 %collective-permute-start.1 = (f32[2,2,3,3,2,1,256]{6,5,4,3,2,1,0:T(1,128)}, f32[2,2,3,3,2,1,256]{6,5,4,3,2,1,0:T(1,128)}, u32[]{:S(2)}, u32[]{:S(2)}) collective-permute-start(f32[2,2,3,3,2,1,256]{6,5,4,3,2,1,0:T(1,128)} %pad_maximum_fusion.16), channel_id=1, source_target_pairs={{1,0},{2,1},{3,2},{4,3},{5,4},{6,5},{7,6},{0,7},{9,8},{10,9},{11,1... | collective-permute-start | bytes 221192 | tf_op jit(solution)/shard_map/ppermute | solution.py:35
  86.0 0.9 mul.1834
  86.9 0.9 mul.1830
  87.9 1.3 dynamic-slice
  89.2 1.3 dynamic-slice.1
  96.4 0.9 mul.1880
  106.8 1.2 fusion.29
  108.0 1.4 dynamic-update-slice
  109.4 1.3 dynamic-slice.2
  110.7 15.4 %all-reduce.1 = f32[8]{0:T(128)S(1)} all-reduce(f32[8]{0:T(128)S(1)} %dynamic-update-slice), channel_id=1, replica_groups=mesh['ta_0'=8,'ta_1'=4,'ta_2'=2,'gz'=8] {'ta_0'}, use_global_device_ids=true, to_apply=%add.1 | all-reduce | flops 8 | bytes 64
  126.7 1.4 dynamic-update-slice.1
  128.1 1.3 dynamic-slice.3
  129.3 10.5 %all-reduce.2 = f32[4]{0:T(128)S(1)} all-reduce(f32[4]{0:T(128)S(1)} %dynamic-update-slice.1), channel_id=1, replica_groups=mesh['ta_0'=8,'ta_1'=4,'ta_2'=2,'gz'=8] {'ta_1'}, use_global_device_ids=true, to_apply=%add.2 | all-reduce | flops 4 | bytes 32
  140.4 1.4 dynamic-update-slice.2
  141.9 2.5 %all-reduce.3 = f32[2]{0:T(128)S(1)} all-reduce(f32[2]{0:T(128)S(1)} %dynamic-update-slice.2), channel_id=1, replica_groups=mesh['ta_0'=8,'ta_1'=4,'ta_2'=2,'gz'=8] {'ta_2'}, use_global_device_ids=true, to_apply=%add.3 | all-reduce | flops 2 | bytes 16
  145.0 1.3 dynamic-update-slice.3
  147.2 15.6 %all-reduce.4 = f32[8]{0:T(128)S(1)} all-reduce(f32[8]{0:T(128)S(1)} %dynamic-update-slice.3), channel_id=1, replica_groups=mesh['ta_0'=8,'ta_1'=4,'ta_2'=2,'gz'=8] {'gz'}, use_global_device_ids=true, to_apply=%add.4 | all-reduce | flops 8 | bytes 64
  (211 shorter events, 45.2 us)
Async XLA Ops:
  0.6 0.9 copy-start.3
  47.8 42.6 %collective-permute-start = (f32[2,3,3,2,1,256]{5,3,2,1,4,0:T(2,128)}, f32[2,3,3,2,1,256]{5,3,2,1,4,0:T(2,128)}, u32[]{:S(2)}, u32[]{:S(2)}) collective-permute-start(f32[2,3,3,2,1,256]{5,3,2,1,4,0:T(2,128)} %pad_maximum_fusion.17), channel_id=1, source_target_pairs={{1,0},{2,1},{3,2},{4,3},{5,4},{6,5},{7,6},{0,7},{9,8},{10,9},{11,1... | collective-permute-start | bytes 110600 | tf_op jit(solution)/shard_map/ppermute | solution.py:35
  60.8 1.0 copy-start.2
  67.4 0.9 copy-start.6
  67.4 0.9 copy-start.7
  68.3 1.2 copy-start.13
  70.7 31.6 %collective-permute-start.1 = (f32[2,2,3,3,2,1,256]{6,5,4,3,2,1,0:T(1,128)}, f32[2,2,3,3,2,1,256]{6,5,4,3,2,1,0:T(1,128)}, u32[]{:S(2)}, u32[]{:S(2)}) collective-permute-start(f32[2,2,3,3,2,1,256]{6,5,4,3,2,1,0:T(1,128)} %pad_maximum_fusion.16), channel_id=1, source_target_pairs={{1,0},{2,1},{3,2},{4,3},{5,4},{6,5},{7,6},{0,7},{9,8},{10,9},{11,1... | collective-permute-start | bytes 221192 | tf_op jit(solution)/shard_map/ppermute | solution.py:35
  78.4 0.9 copy-start.15
  78.4 0.9 copy-start.16
  81.0 0.9 copy-start.14
  86.9 4.4 %copy-start.12 = (f32[3,3,2,3,256]{4,3,1,0,2:T(4,128)S(1)}, f32[3,3,2,3,256]{4,3,1,0,2:T(4,128)}, u32[]{:S(2)}) copy-start(f32[3,3,2,3,256]{4,3,1,0,2:T(4,128)} %fusion.1) | copy-start | bytes 165892
  91.3 0.9 copy-start.4
  91.3 0.9 copy-start.5
  97.5 1.1 copy-start
  97.5 1.1 copy-start.28
  99.5 0.9 copy-start.19
  100.4 0.9 copy-start.10
  100.4 0.9 copy-start.11
  101.3 0.9 copy-start.17
  101.3 0.9 copy-start.18
  102.4 0.9 copy-start.22
  103.3 0.9 copy-start.21
  105.0 0.9 copy-start.9
  141.9 4.4 %copy-start.1 = (f32[1,2,3,3,2,4,256]{6,5,4,3,2,1,0:T(4,128)S(1)}, f32[1,2,3,3,2,4,256]{6,5,4,3,2,1,0:T(4,128)}, u32[]{:S(2)}) copy-start(f32[1,2,3,3,2,4,256]{6,5,4,3,2,1,0:T(4,128)} %maximum_bitcast_fusion) | copy-start | bytes 442372
  (7 other events, 5.6 us)
